TPU v7x, 128 devices: a whole 4x4x4 slice. The times are simulated.
128 devices in a mesh: res: 4 (over x_hi, core), blk: 32 (over x_lo, y, z).
Axes of the slice: x: 4 (x_hi: 2, x_lo: 2; x = x_hi * 2 + x_lo), y: 4, z: 4, core: 2. Of those that a mesh axis runs over, the one named last changes fastest.
Arguments:
- modes: float32 [2, 8, 4194304], P(None, 'res', 'blk'), may hold values from -0.078125 to 0.078125
Outputs:
- product_modes: float32 [2, 8, 4194304], P(None, 'res', 'blk')
All inputs are finite; a program needn't handle non-finite values.
Results may differ from a plain program's by a relative error of at most 0.000098.
Values sent between devices are 32-bit elements; how exact they have to be, the bound alone decides.
A program may use at most 128 MiB of HBM per device.

v0:
```python
import math

import jax
import jax.numpy as jnp
from jax import lax
from jax.sharding import Mesh
from jax.sharding import PartitionSpec as P

INNER = 512
EIGHTH = 4194304
SUBLEN = 12582912
PADDED = 50331648
RES = ("res_0", "res_1")


highest = lax.Precision.HIGHEST


def own_block(tiles, axes, order):
    lengths = [lax.axis_size(a) for a in axes]
    tiles = tiles.reshape(*lengths, *tiles.shape[1:])
    tiles = tiles.transpose(*order, *range(len(axes), tiles.ndim))
    tiles = tiles.reshape(-1, *tiles.shape[len(axes) :])
    for k in order:
        tiles = lax.psum_scatter(tiles, axes[k], scatter_dimension=0, tiled=True)
    return tiles[0]


def split_up(x, dim, length):
    lengths = x.shape
    tiles = x.reshape(*lengths[:dim], length, lengths[dim] // length, *lengths[dim + 1 :])
    return jnp.moveaxis(tiles, dim, 0)


def sum_by_axis(x, axes, order, dim):
    length = lax.axis_size(axes)
    return own_block(split_up(x, dim, length), axes, order)


def grid_index(shape, axis_number):
    return lax.broadcasted_iota(jnp.int32, shape, axis_number)


def rotation(position, period, direction, factor):
    angle = direction * 2.0 * math.pi / period * (position % period).astype(jnp.float32)
    return jnp.stack([factor * jnp.cos(angle), factor * jnp.sin(angle)])


def times(left, right):
    return jnp.stack(
        [left[0] * right[0] - left[1] * right[1], left[0] * right[1] + left[1] * right[0]]
    )


def table_pair(length):
    rows = grid_index((length, length), 0)
    columns = grid_index((length, length), 1)
    angle = 2.0 * math.pi / length * (rows * columns % length).astype(jnp.float32)
    cosine = jnp.cos(angle)
    sine = jnp.sin(angle)
    forward = jnp.stack([jnp.stack([cosine, -sine], 1), jnp.stack([sine, cosine], 1)])
    backward = jnp.stack([jnp.stack([cosine, sine], 1), jnp.stack([-sine, cosine], 1)])
    return (forward, backward)


def fold_eighths(every, residue):
    parity = residue % 2
    quarter = jnp.stack([(1 - parity) * (1 - residue), parity * (2 - residue)]).astype(jnp.float32)
    quarter = quarter.reshape((2,) + (1,) * (every.ndim - 1))
    flipped = (1 - 2 * parity).astype(jnp.float32)
    padding = jnp.zeros_like(every[:, 0:1])
    upper = jnp.concatenate([every[:, 6:8], padding], axis=1)
    return every[:, 0:3] + times(quarter, every[:, 3:6]) + flipped * upper


def on_device(modes):
    width = modes.shape[2]
    blocks = lax.axis_size("blk")
    block = lax.axis_index("blk")
    residue = lax.axis_index(RES)
    narrow = width // blocks
    outer = width // INNER
    first_len = 3 * blocks
    first_pair = table_pair(first_len)
    outer_pair = table_pair(outer)
    inner_pair = table_pair(INNER)
    moved_in = lax.all_to_all(
        modes.reshape(2, 2, blocks, narrow), "blk", split_axis=2, concat_axis=2, tiled=True
    )
    every = lax.all_gather(moved_in, RES, axis=1, tiled=True)
    shape = (3, blocks, narrow)
    position = (
        EIGHTH * grid_index(shape, 0)
        + width * grid_index(shape, 1)
        + block * narrow
        + grid_index(shape, 2)
    )
    spread = times(rotation(residue * position, PADDED, 1.0, 1.0), fold_eighths(every, residue))
    gathered = spread.reshape(2, first_len, narrow)
    section = jnp.einsum("akbj,bjr->akr", first_pair[0], gathered, precision=highest)
    freq_ids = grid_index((first_len, narrow), 0)
    column_ids = block * narrow + grid_index((first_len, narrow), 1)
    section = times(rotation(freq_ids * column_ids, SUBLEN, 1.0, 1.0), section)
    back = lax.all_to_all(
        section.reshape(2, blocks, 3, narrow), "blk", split_axis=1, concat_axis=3, tiled=True
    )
    local = back.reshape(2, 3, outer, INNER)
    local = jnp.einsum("asbp,bxpc->axsc", outer_pair[0], local, precision=highest)
    inner_turn = rotation(
        grid_index((outer, INNER), 0) * grid_index((outer, INNER), 1), width, 1.0, 1.0
    )
    inner_turn = inner_turn.reshape(2, 1, outer, INNER)
    local = times(inner_turn, local)
    values = jnp.einsum("akbj,bxsj->axsk", inner_pair[0], local, precision=highest)
    squared = jnp.stack(
        [values[0] * values[0] - values[1] * values[1], 2.0 * values[0] * values[1]]
    )
    local = jnp.einsum("akbj,bxsj->axsk", inner_pair[1], squared, precision=highest)
    local = times(jnp.stack([inner_turn[0], -inner_turn[1]]), local)
    local = jnp.einsum("asbp,bxpc->axsc", outer_pair[1], local, precision=highest).reshape(
        2, 3, width
    )
    slab_ids = 3 * block + grid_index((3, width), 0)
    local = times(rotation(slab_ids * grid_index((3, width), 1), SUBLEN, -1.0, 1.0), local)
    moved = lax.all_to_all(
        local.reshape(2, 3, blocks, narrow), "blk", split_axis=2, concat_axis=1, tiled=True
    )
    inverted = jnp.einsum(
        "akbj,bjr->akr", first_pair[1], moved.reshape(2, first_len, narrow), precision=highest
    )
    arranged = inverted.reshape(2, 3, blocks, narrow)
    picked = jnp.concatenate([arranged[:, 1:3], arranged, arranged], axis=1)
    shape = (8, blocks, narrow)
    place = (
        (grid_index(shape, 0) + 4) * EIGHTH
        + width * grid_index(shape, 1)
        + block * narrow
        + grid_index(shape, 2)
    )
    partial_value = times(rotation(residue * place, PADDED, -1.0, 1.0 / PADDED), picked)
    reduced = sum_by_axis(partial_value, RES, (1, 0), 1)
    owned = lax.all_to_all(reduced, "blk", split_axis=2, concat_axis=3, tiled=True)
    return owned.reshape(2, 2, width)


def solution(mesh):
    finer = Mesh(mesh.devices.reshape(2, 2, mesh.shape["blk"]), ("res_0", "res_1", "blk"))
    placed = (P(None, RES, "blk"),)
    return jax.shard_map(
        on_device, mesh=finer, in_specs=placed, out_specs=P(None, RES, "blk"), check_vma=False
    )
```

profile of v0, /device:TPU:0, one launch (start us, length us, event | category | flops | bytes accessed | tf_op | source)
XLA Modules:
  0.0 475.4 jit_solution(14859076652628164501)
XLA Ops:
  6.5 1.7 copy.79
  8.3 36.9 %all_to_all.44 = f32[2,2,32,4096]{3,1,0,2:T(2,128)S(1)} all-to-all(f32[2,2,32,4096]{3,1,0,2:T(2,128)S(1)} %bitcast.135), channel_id=1, replica_groups=mesh['res_0'=2,'res_1'=2,'blk'=32] {'blk'}, dimensions={2} | all-to-all | bytes 4194304 | tf_op jit(solution)/shard_map/all_to_all | solution.py:87
  45.2 2.5 copy.40
  47.9 0.7 fusion.123
  49.0 59.3 %all-gather.2.cloned.1.call-done = f32[2,8,32,4096]{3,2,1,0:T(8,128)} async-done(((f32[2,2,32,4096]{3,2,1,0:T(8,128)}), f32[2,8,32,4096]{3,2,1,0:T(8,128)}) %all-gather.2.cloned.1.call-update) | async-done | bytes 8388624 | tf_op jit(solution)/shard_map/all_gather | solution.py:90
  108.3 4.9 %multiply_subtract_fusion.7 = (f32[1,3,32,4096]{3,2,1,0:T(8,128)S(1)}, f32[1,3,32,4096]{3,2,1,0:T(8,128)S(1)}) fusion(f32[2,8,32,4096]{3,2,1,0:T(8,128)} %all-gather.2.cloned.1.call-done, f32[]{:T(128)} %bitcast.5, f32[]{:T(128)} %bitcast.4), kind=kLoop, calls=%fused_computation.81 | loop fusion | flops 2359296 | bytes 6291464 | tf_op jit(solution)/shard_map/sub | solution.py:51
  113.2 0.7 fusion.11
  114.0 6.8 %multiply_subtract_fusion.6 = (f32[1,3,32,4096]{3,2,1,0:T(8,128)S(1)}, f32[1,3,32,4096]{3,2,1,0:T(8,128)S(1)}) fusion(f32[2,3,32,4096]{3,2,1,0:T(8,128)S(1)} %fusion.11, s32[]{:T(128)S(6)} %mul.717, s32[32]{0:T(128)S(1)} %iota_multiply_fusion.1, s32[3]{0:T(128)S(1)} %iota_multiply_fusion, s32[]{:T(128)S(6)} %add.397), kind=kLoop, calls=%fused_computation.79 | loop fusion | flops 7077888 | bytes 6291604 | tf_op jit(solution)/shard_map/sub | solution.py:51
  120.8 3.0 convolution_bitcast_fusion.1
  123.8 6.9 %multiply_subtract_fusion.5 = (f32[1,96,4096]{2,1,0:T(8,128)S(1)}, f32[1,96,4096]{2,1,0:T(8,128)S(1)}) fusion(f32[2,96,4096]{2,1,0:T(8,128)S(1)} %convolution_bitcast_fusion.1, s32[4096]{0:T(1024)S(1)} %iota_add_fusion), kind=kLoop, calls=%fused_computation.77 | loop fusion | flops 5898240 | bytes 6307840 | tf_op jit(solution)/shard_map/sub | solution.py:51
  130.8 3.1 stack.189
  133.8 3.0 stack.190
  136.9 6.2 %pad_maximum_fusion.2 = f32[2,32,3,4096]{3,0,2,1:T(2,128)} fusion(f32[1,32,3,4096]{3,0,2,1:T(1,128)} %stack.190, f32[1,32,3,4096]{3,0,2,1:T(1,128)S(1)} %copy-done.1), kind=kLoop, calls=%fused_computation.28 | loop fusion | flops 786432 | bytes 6291456 | tf_op jit(solution)/shard_map/stack | solution.py:50
  143.1 7.3 %all-to-all-start.1 = ((f32[2,32,3,4096]{3,0,2,1:T(2,128)}), f32[2,32,3,4096]{3,0,2,1:T(2,128)S(1)}, u32[]{:S(2)}, u32[]{:S(2)}) async-start(f32[2,32,3,4096]{3,0,2,1:T(2,128)} %pad_maximum_fusion.2), calls=%async_computation.1 | async-start | bytes 6291456 | tf_op jit(solution)/shard_map/all_to_all | solution.py:104
  150.4 1.0 fusion.99
  151.3 1.0 fusion.97
  152.4 2.7 fusion.86
  155.1 3.3 fusion.83
  158.3 3.9 fusion.77
  162.2 4.1 fusion.72
  166.3 1.4 fusion.68
  167.7 4.0 fusion.26
  171.7 18.5 %all-to-all-done.1 = f32[2,32,3,4096]{3,0,2,1:T(2,128)S(1)} async-done(((f32[2,32,3,4096]{3,0,2,1:T(2,128)}), f32[2,32,3,4096]{3,0,2,1:T(2,128)S(1)}, u32[]{:S(2)}, u32[]{:S(2)}) %all-to-all-start.1) | async-done | bytes 3145760 | tf_op jit(solution)/shard_map/all_to_all | solution.py:104
  190.2 3.5 copy.41
  193.7 3.0 reshape.591
  196.7 11.6 %fusion.28 = f32[2,3,256,512]{2,3,0,1:T(8,128)S(1)} fusion(f32[1,256,2,256]{3,1,2,0:T(8,128)} %get-tuple-element.30, f32[1,256,2,256]{3,1,2,0:T(8,128)} %get-tuple-element.33, f32[2,3,256,512]{3,2,1,0:T(8,128)S(1)} %reshape.591), kind=kOutput, calls=%fused_computation.55 | convolution fusion | flops 4832100352 | bytes 7340032 | tf_op jit(solution)/shard_map/asbp,bxpc->axsc/dot_general | solution.py:108
  208.8 1.2 copy-done.9
  210.6 20.9 %fusion.33 = f32[2,3,256,512]{3,2,0,1:T(8,128)S(1)} fusion(f32[1,512,2,512]{3,1,2,0:T(8,128)S(1)} %copy-done.10, f32[1,512,2,512]{3,1,2,0:T(8,128)S(1)} %copy-done.9, f32[1,3,256,512]{2,3,0,1:T(8,128)S(1)} %get-tuple-element.12, f32[1,3,256,512]{2,3,0,1:T(8,128)S(1)} %get-tuple-element.11), kind=kOutput, calls=%fused_computation.58 | convolution fusion | flops 9665511424 | bytes 10485760 | tf_op jit(solution)/shard_map/akbj,bxsj->axsk/dot_general | solution.py:114
  232.0 1.1 copy-done.7
  233.7 10.6 %fusion.32 = f32[2,3,256,512]{2,3,0,1:T(8,128)S(1)} fusion(f32[1,512,2,512]{3,1,2,0:T(8,128)S(1)} %copy-done.7, f32[1,512,2,512]{3,1,2,0:T(8,128)S(1)} %copy-done.8, f32[1,3,256,512]{3,2,0,1:T(8,128)S(1)} %get-tuple-element.22, f32[1,3,256,512]{3,2,0,1:T(8,128)S(1)} %get-tuple-element.21), kind=kOutput, calls=%fused_computation.57 | convolution fusion | flops 9665511424 | bytes 10485760 | tf_op jit(solution)/shard_map/akbj,bxsj->axsk/dot_general | solution.py:118
  245.5 5.4 %fusion.31 = f32[2,3,256,512]{2,3,0,1:T(8,128)S(1)} fusion(f32[1,3,256,512]{2,3,0,1:T(8,128)S(1)} %get-tuple-element.10, f32[1,3,256,512]{2,3,0,1:T(8,128)S(1)} %get-tuple-element.9, f32[1,256,2,256]{3,1,2,0:T(8,128)S(1)} %copy-done.6, f32[1,256,2,256]{3,1,2,0:T(8,128)S(1)} %copy-done.5), kind=kOutput, calls=%fused_computation.56 | convolution fusion | flops 4832886784 | bytes 7340032 | tf_op jit(solution)/shard_map/asbp,bxpc->axsc/dot_general | solution.py:120
  250.9 1.5 fusion.122
  253.2 1.9 copy.46
  255.1 1.4 squeeze.7
  256.5 8.4 %multiply_subtract_fusion.1 = (f32[1,3,32,4096]{3,2,1,0:T(8,128)S(1)}, f32[1,3,32,4096]{3,2,1,0:T(8,128)S(1)}) fusion(f32[1,3,32,4096]{3,2,1,0:T(8,128)} %squeeze.7, f32[1,3,32,4096]{3,2,1,0:T(8,128)S(1)} %squeeze.6, s32[3]{0:T(128)S(1)} %iota_add_fusion.1), kind=kLoop, calls=%fused_computation.66 | loop fusion | flops 6684672 | bytes 6291468 | tf_op jit(solution)/shard_map/sub | solution.py:51
  265.1 4.1 copy.47
  269.2 8.4 %all-to-all-start.2 = ((f32[2,3,32,4096]{3,0,1,2:T(2,128)}), f32[2,3,32,4096]{3,0,1,2:T(2,128)S(1)}, u32[]{:S(2)}, u32[]{:S(2)}) async-start(f32[2,3,32,4096]{3,0,1,2:T(2,128)} %copy.47), calls=%async_computation.2 | async-start | bytes 6291456 | tf_op jit(solution)/shard_map/all_to_all | solution.py:125
  277.9 39.0 %all-to-all-done.2 = f32[2,3,32,4096]{3,0,1,2:T(2,128)S(1)} async-done(((f32[2,3,32,4096]{3,0,1,2:T(2,128)}), f32[2,3,32,4096]{3,0,1,2:T(2,128)S(1)}, u32[]{:S(2)}, u32[]{:S(2)}) %all-to-all-start.2) | async-done | bytes 3145760 | tf_op jit(solution)/shard_map/all_to_all | solution.py:125
  317.0 4.5 convolution_bitcast_fusion
  321.7 0.9 pad_maximum_fusion
  322.6 18.4 %multiply_subtract_fusion = (f32[1,8,32,4096]{3,2,1,0:T(8,128)S(1)}, f32[1,8,32,4096]{3,2,1,0:T(8,128)S(1)}) fusion(f32[2,8,32,4096]{3,2,1,0:T(8,128)S(1)} %pad_maximum_fusion, s32[]{:T(128)S(6)} %mul.717, s32[32]{0:T(128)S(1)} %iota_multiply_fusion.1, s32[8]{0:T(128)S(1)} %add_multiply_fusion, s32[]{:T(128)S(6)} %add.397), kind=kLoop, calls=%fused_computation.16 | loop fusion | flops 20971520 | bytes 16777384 | tf_op jit(solution)/shard_map/sub | solution.py:51
  340.9 1.0 pad_maximum_fusion.1
  341.9 3.8 copy.49
  345.8 21.1 %reduce-scatter.3.cloned.1.call-done = f32[2,2,2,32,4096]{4,3,2,1,0:T(8,128)} async-done(((f32[4,2,2,32,4096]{4,3,2,1,0:T(8,128)}), f32[2,2,2,32,4096]{4,3,2,1,0:T(8,128)}) %reduce-scatter.3.cloned.1.call-update) | async-done | bytes 4194320 | tf_op jit(solution)/shard_map/reduce_scatter | solution.py:25
  367.0 62.2 %reduce-scatter.5.cloned.1.call-done = f32[1,2,2,32,4096]{4,3,2,1,0:T(8,128)} async-done(((f32[2,2,2,32,4096]{4,3,2,1,0:T(8,128)}), f32[1,2,2,32,4096]{4,3,2,1,0:T(8,128)}) %reduce-scatter.5.cloned.1.call-update) | async-done | bytes 2097168 | tf_op jit(solution)/shard_map/reduce_scatter | solution.py:25
  429.2 3.2 copy.50
  432.4 34.6 %all_to_all.45 = f32[2,2,32,4096]{3,1,0,2:T(2,128)S(1)} all-to-all(f32[2,2,32,4096]{3,1,0,2:T(2,128)S(1)} %copy.50), channel_id=1, replica_groups=mesh['res_0'=2,'res_1'=2,'blk'=32] {'blk'}, dimensions={2} | all-to-all | bytes 4194304 | tf_op jit(solution)/shard_map/all_to_all | solution.py:142
  466.9 1.5 copy.71
  (46 shorter events, 5.5 us)
Async XLA Ops:
  6.5 101.7 %all-gather.2.cloned.1.call-start = ((), (), s32[]{:S(2)}) async-start(), calls=%async_computation.6 | async-start | bytes 10485760 | tf_op jit(solution)/shard_map/all_gather | solution.py:90
  108.3 4.9 %copy-start = (f32[2,8,32,4096]{3,2,1,0:T(8,128)S(1)}, f32[2,8,32,4096]{3,2,1,0:T(8,128)}, u32[]{:S(2)}) copy-start(f32[2,8,32,4096]{3,2,1,0:T(8,128)} %all-gather.2.cloned.1.call-done) | copy-start | bytes 25165828
  108.3 4.9 %slice-start = ((f32[2,8,32,4096]{3,2,1,0:T(8,128)}), f32[2,2,32,4096]{3,2,1,0:T(8,128)S(1)}, s32[]{:S(2)}) async-start(f32[2,8,32,4096]{3,2,1,0:T(8,128)} %all-gather.2.cloned.1.call-done), calls=%async_computation.9 | async-start | bytes 4194304 | tf_op jit(solution)/shard_map/slice | solution.py:72
  133.8 3.0 copy-start.1
  143.1 47.1 %all-to-all-start.1 = ((f32[2,32,3,4096]{3,0,2,1:T(2,128)}), f32[2,32,3,4096]{3,0,2,1:T(2,128)S(1)}, u32[]{:S(2)}, u32[]{:S(2)}) async-start(f32[2,32,3,4096]{3,0,2,1:T(2,128)} %pad_maximum_fusion.2), calls=%async_computation.1 | async-start | bytes 6291456 | tf_op jit(solution)/shard_map/all_to_all | solution.py:104
  196.7 11.6 %copy-start.2 = (f32[256,512]{0,1:T(8,128)S(1)}, f32[256,512]{0,1:T(8,128)}, u32[]{:S(2)}) copy-start(f32[256,512]{0,1:T(8,128)} %get-tuple-element.49) | copy-start | bytes 1572868
  196.7 11.6 %copy-start.4 = (f32[256,512]{0,1:T(8,128)S(1)}, f32[256,512]{0,1:T(8,128)}, u32[]{:S(2)}) copy-start(f32[256,512]{0,1:T(8,128)} %get-tuple-element.48) | copy-start | bytes 1572868
  208.4 1.6 copy-start.9
  208.4 2.2 copy-start.10
  231.5 1.6 copy-start.7
  231.5 2.2 copy-start.8
  233.7 10.6 %copy-start.3 = (f32[256,512]{0,1:T(8,128)S(1)}, f32[256,512]{0,1:T(8,128)}, u32[]{:S(2)}) copy-start(f32[256,512]{0,1:T(8,128)} %fusion.86) | copy-start | bytes 1572868
  244.3 1.0 copy-start.5
  244.3 1.2 copy-start.6
  269.2 47.8 %all-to-all-start.2 = ((f32[2,3,32,4096]{3,0,1,2:T(2,128)}), f32[2,3,32,4096]{3,0,1,2:T(2,128)S(1)}, u32[]{:S(2)}, u32[]{:S(2)}) async-start(f32[2,3,32,4096]{3,0,1,2:T(2,128)} %copy.47), calls=%async_computation.2 | async-start | bytes 6291456 | tf_op jit(solution)/shard_map/all_to_all | solution.py:125
  277.6 89.4 %reduce-scatter.3.cloned.1.call-start = ((), (), s32[]{:S(2)}) async-start(), calls=%async_computation.7 | async-start | bytes 12582912 | tf_op jit(solution)/shard_map/reduce_scatter | solution.py:25
  345.8 83.4 %reduce-scatter.5.cloned.1.call-start = ((), (), s32[]{:S(2)}) async-start(), calls=%async_computation.8 | async-start | bytes 6291456 | tf_op jit(solution)/shard_map/reduce_scatter | solution.py:25
Sparse Core Ops, SparseCore 0:
  47.9 60.3 all-gather.1
  345.9 21.0 reduce-scatter.2
  369.3 59.7 reduce-scatter.4
where the time goes:
time: 485 us; the launch traced here: 475 us
  waiting for transfers between devices  200 us (41%)
  other arithmetic  77.8 us (16%)
  blocking collectives  71.5 us (15%)
  matrix products  56 us (12%)
  local copies, waits for them, and re-layouts  40.2 us (8%)
  starting transfers between devices  15.7 us (3%)
  between operations  14 us (3%)
    reduce_scatter x2, waiting for transfers between devices, own_block(): tiles = lax.psum_scatter(tiles, axes[k], scatter_dimension=0, tiled=True)  83.3 us
    all_gather x1, waiting for transfers between devices, on_device(): every = lax.all_gather(moved_in, RES, axis=1, tiled=True)  59.3 us
    sub x7, other arithmetic, times(): left[0] * right[0] - left[1] * right[1]  46.1 us
    all_to_all x1, waiting for transfers between devices, on_device(): lax.all_to_all(local.reshape(2, 3, blocks, narrow), 'blk', split_axis=2,...  39 us
    all_to_all x1, blocking collectives, on_device(): lax.all_to_all(modes.reshape(2, 2, blocks, narrow), 'blk', split_axis=2,...  36.9 us
    all_to_all x1, blocking collectives, on_device(): lax.all_to_all(reduced, 'blk', split_axis=2, concat_axis=3, tiled=True)  34.6 us
    dot_general x1, matrix products, on_device(): jnp.einsum('akbj,bxsj->axsk', inner_pair[0], local, precision=highest)  20.9 us
    all_to_all x1, waiting for transfers between devices, on_device(): lax.all_to_all(section.reshape(2, blocks, 3, narrow), 'blk', split_axis=1...  18.5 us
  transfers between devices with their start and end apart: 5, of which 5 were waited for; matrix products, arithmetic and copies ran while one was open for 5% of the time, Pallas kernels for 0%

commit v1 on v0

v1 whole, which is shorter than its diff:
```python
import math

import jax
import jax.numpy as jnp
import numpy as np
from jax import lax
from jax.experimental import pallas as pl
from jax.experimental.pallas import tpu as pltpu
from jax.sharding import PartitionSpec as P

F32, BF16 = jnp.float32, jnp.bfloat16
DEVICES = 128
PADDED = 50331648
LOCAL = 131072
STEP = 37
MESH = pl.DeviceIdType.MESH
HALF_ROOT3 = math.sqrt(3.0) / 2.0
ROOT_HALF = math.sqrt(0.5)


def real_block(w):
    return np.block([[w.real, -w.imag], [w.imag, w.real]])


def high_low(w):
    high = np.asarray(w, np.float32).astype(jnp.bfloat16)
    low = (w - high.astype(np.float64)).astype(np.float32).astype(jnp.bfloat16)
    return np.stack([high, low])


def root(turns):
    return np.exp(2j * np.pi * (turns % 1.0))


def tables():
    n = np.arange(128)
    kl = np.array([(u // 32) * 64 + e * 32 + u % 32 for e in range(2) for u in range(64)])
    first, last = [], []
    for s in range(3):
        w = root(np.outer(n, kl) / 128.0) * root(kl * s / 384.0)[None, :]
        first.append(high_low(real_block(w)))
        last.append(high_low(real_block(w).T / PADDED))
    f = real_block(root(np.outer(n, n) / 128.0))
    turn = [root(np.outer(3 * n + s, n) / PADDED) for s in range(3)]
    turn.append(root(np.outer(n, n) / 16384.0))
    columns = np.zeros((128, 128), np.complex128)
    columns[:, :8] = root(np.outer(n, np.arange(8)) / 1024.0)
    turn.append(columns)
    rows = np.zeros((128, 128), np.complex128)
    rows[:8] = root(np.outer(np.arange(8), n) / LOCAL)
    turn.append(rows)
    turn = np.stack([np.stack([t.real, t.imag]) for t in turn]).astype(np.float32)
    return (
        np.stack(first),
        np.stack(last),
        np.stack([high_low(f), high_low(f.T)]),
        turn,
    )


def split(x):
    high = x.astype(BF16)
    return high, (x - high.astype(F32)).astype(BF16)


def dot(a, b):
    return jnp.dot(a, b, preferred_element_type=F32)


def left(w_high, w_low, x):
    high, low = split(x)
    return dot(w_high, high) + dot(w_high, low) + dot(w_low, high)


def right(x, w_high, w_low):
    high, low = split(x)
    return dot(high, w_high) + dot(low, w_high) + dot(high, w_low)


def times(a, b):
    return a[0] * b[0] - a[1] * b[1], a[0] * b[1] + a[1] * b[0]


def times_conj(a, b):
    return a[0] * b[0] + a[1] * b[1], a[1] * b[0] - a[0] * b[1]


def add(a, b):
    return a[0] + b[0], a[1] + b[1]


def sub(a, b):
    return a[0] - b[0], a[1] - b[1]


def quarter(a, sign):
    return (-a[1], a[0]) if sign > 0 else (a[1], -a[0])


def eighth(a, sign):
    if sign > 0:
        return (a[0] - a[1]) * ROOT_HALF, (a[0] + a[1]) * ROOT_HALF
    return (a[0] + a[1]) * ROOT_HALF, (a[1] - a[0]) * ROOT_HALF


def four(a, b, c, d, sign):
    p, q, r, t = add(a, c), sub(a, c), add(b, d), quarter(sub(b, d), sign)
    return add(p, r), add(q, t), sub(p, r), sub(q, t)


def eight(v, sign):
    even = four(v[0], v[2], v[4], v[6], sign)
    odd = four(v[1], v[3], v[5], v[7], sign)
    odd = (
        odd[0],
        eighth(odd[1], sign),
        quarter(odd[2], sign),
        quarter(eighth(odd[3], sign), sign),
    )
    return [add(e, o) for e, o in zip(even, odd)] + [sub(e, o) for e, o in zip(even, odd)]


def kernel(
    x_ref, first_hbm, last_hbm, fg_hbm, turn_hbm, o_ref,
    first, last, fg, turn, got1, put2, got2, put3, got3, put4,
    outer_turn, column_turn, inner_turn, high, low, back, held,
    const_sem, own_sem, send1, recv1, send2, recv2, send3, recv3, send4, recv4,
):
    r, b = lax.axis_index("res"), lax.axis_index("blk")
    me = r * 32 + b

    constants = [
        pltpu.make_async_copy(src, dst, const_sem.at[i])
        for i, (src, dst) in enumerate(
            ((first_hbm, first), (last_hbm, last), (fg_hbm, fg), (turn_hbm, turn))
        )
    ]
    for copy in constants:
        copy.start()
    own_in = pltpu.make_async_copy(x_ref.at[:, me], got1.at[:, :, me], own_sem.at[0])
    own_in.start()

    def everyone(body):
        def step(i, carry):
            to = (me + i * STEP) % DEVICES
            body(to, {"res": to // 32, "blk": to % 32})
            return carry

        lax.fori_loop(1, DEVICES, step, 0)

    barrier = pltpu.get_barrier_semaphore()
    everyone(
        lambda to, device: pl.semaphore_signal(
            barrier, inc=1, device_id=device, device_id_type=MESH
        )
    )
    pl.semaphore_wait(barrier, DEVICES - 1)

    def remote(src, dst, send, recv, device):
        return pltpu.make_async_remote_copy(
            src_ref=src,
            dst_ref=dst,
            send_sem=send,
            recv_sem=recv,
            device_id=device,
            device_id_type=MESH,
        )

    def here(src, dst, send, recv):
        return remote(src, dst, send, recv, {"res": r, "blk": b})

    everyone(
        lambda to, device: remote(
            x_ref.at[:, to], got1.at[:, :, me], send1, recv1, device
        ).start()
    )

    for copy in constants:
        copy.wait()

    n1 = lax.broadcasted_iota(jnp.int32, (128, 128), 0)
    lane = lax.broadcasted_iota(jnp.int32, (128, 128), 1)
    angle = ((8 * me + lane % 8) * (3 * n1 + lane // 8)).astype(F32) * (
        2.0 * math.pi * 128.0 / PADDED
    )
    cosine, sine = jnp.cos(angle), jnp.sin(angle)
    for s in range(3):
        for s8 in range(8):
            at = 8 * s + s8
            column = (
                jnp.broadcast_to(cosine[:, at : at + 1], (128, 128)),
                jnp.broadcast_to(sine[:, at : at + 1], (128, 128)),
            )
            re, im = times(column, (turn[s, 0], turn[s, 1]))
            outer_turn[s, s8, 0] = re
            outer_turn[s, s8, 1] = im
    for a in range(8):
        for part in range(2):
            column_turn[a, part] = jnp.broadcast_to(turn[4, part, :, a : a + 1], (128, 128))
        row = (
            jnp.broadcast_to(turn[5, 0, a : a + 1, :], (128, 128)),
            jnp.broadcast_to(turn[5, 1, a : a + 1, :], (128, 128)),
        )
        re, im = times(row, (turn[3, 0], turn[3, 1]))
        inner_turn[a, 0] = re
        inner_turn[a, 1] = im

    own_in.wait()
    some = pl.ds(0, DEVICES - 1)
    here(x_ref.at[:, some], got1.at[:, :, some], send1, recv1).wait_recv()

    rows1 = got1.reshape(2 * 2 * 128 * 8, 128)
    rows2 = put2.reshape(3 * 2 * 128 * 8, 128)
    rows3 = got3.reshape(3 * 2 * 128 * 8, 128)
    rows4 = put4.reshape(2 * 2 * 128 * 8, 128)

    def outer_forward(s):
        cr = (1.0, -0.5, -0.5)[s]
        ci = (0.0, HALF_ROOT3, -HALF_ROOT3)[s]

        def body(h, carry):
            columns = []
            for j in range(2):
                def block(part, upper):
                    at = ((part * 2 + h // 2) * 128 + upper * 64) * 8 + ((h % 2) * 2 + j) * 2
                    return jnp.concatenate(
                        [rows1[pl.ds(at + e, 64, stride=8), :] for e in range(2)], axis=0
                    )

                x0, x1 = (block(0, 0), block(1, 0)), (block(0, 1), block(1, 1))
                if s == 0:
                    y = add(x0, x1)
                else:
                    y = (
                        x0[0] + cr * x1[0] - ci * x1[1],
                        x0[1] + cr * x1[1] + ci * x1[0],
                    )
                columns.append(jnp.concatenate(y, axis=0))
            out = left(first[s, 0], first[s, 1], jnp.concatenate(columns, axis=1))
            for j in range(2):
                s8 = 2 * h + j
                part = (out[:128, 128 * j : 128 * j + 128], out[128:, 128 * j : 128 * j + 128])
                re, im = times(part, (outer_turn[s, s8, 0], outer_turn[s, s8, 1]))
                rows2[pl.ds((s * 2) * 1024 + s8, 128, stride=8), :] = re
                rows2[pl.ds((s * 2 + 1) * 1024 + s8, 128, stride=8), :] = im
            return carry

        lax.fori_loop(0, 4, body, 0)

    mine = pl.ds(pl.multiple_of(8 * me, 8), 8)
    for s in range(3):
        outer_forward(s)
        got2[s, :, mine, :] = put2[s, :, me]
        everyone(
            lambda to, device: remote(
                put2.at[s, :, to], got2.at[s, :, mine, :], send2.at[s], recv2.at[s], device
            ).start()
        )

    def inner(s):
        def open_eight(i, carry):
            at = pl.multiple_of(16 * i, 16)
            v = [
                (got2[s, 0, pl.ds(128 * a + at, 16), :], got2[s, 1, pl.ds(128 * a + at, 16), :])
                for a in range(8)
            ]
            for a, y in enumerate(eight(v, 1)):
                if a:
                    y = times(y, (column_turn[a, 0, pl.ds(at, 16), :], column_turn[a, 1, pl.ds(at, 16), :]))
                for part in range(2):
                    up, down = split(y[part])
                    high[a, pl.ds(128 * part + at, 16), :] = up
                    low[a, pl.ds(128 * part + at, 16), :] = down
            return carry

        lax.fori_loop(0, 8, open_eight, 0)

        def middle(h, carry):
            pair = (2 * h, 2 * h + 1)
            up = jnp.concatenate([high[a] for a in pair], axis=1)
            down = jnp.concatenate([low[a] for a in pair], axis=1)
            out = dot(fg[0, 0], up) + dot(fg[0, 0], down) + dot(fg[0, 1], up)
            lines = []
            for j, a in enumerate(pair):
                y = (out[:128, 128 * j : 128 * j + 128], out[128:, 128 * j : 128 * j + 128])
                lines.append(jnp.concatenate(times(y, (inner_turn[a, 0], inner_turn[a, 1])), axis=1))
            v = right(jnp.concatenate(lines, axis=0), fg[1, 0], fg[1, 1])
            re, im = v[:, :128], v[:, 128:]
            squared = jnp.concatenate([(re + im) * (re - im), 2.0 * re * im], axis=1)
            v = right(squared, fg[0, 0], fg[0, 1])
            columns = []
            for j, a in enumerate(pair):
                y = (v[128 * j : 128 * j + 128, :128], v[128 * j : 128 * j + 128, 128:])
                columns.append(
                    jnp.concatenate(times_conj(y, (inner_turn[a, 0], inner_turn[a, 1])), axis=0)
                )
            out = left(fg[1, 0], fg[1, 1], jnp.concatenate(columns, axis=1))
            for j, a in enumerate(pair):
                y = (out[:128, 128 * j : 128 * j + 128], out[128:, 128 * j : 128 * j + 128])
                re, im = times_conj(y, (column_turn[a, 0], column_turn[a, 1]))
                back[a, 0] = re
                back[a, 1] = im
            return carry

        lax.fori_loop(0, 4, middle, 0)

        def close_eight(i, carry):
            at = pl.multiple_of(16 * i, 16)
            v = [(back[a, 0, pl.ds(at, 16), :], back[a, 1, pl.ds(at, 16), :]) for a in range(8)]
            for a, y in enumerate(eight(v, -1)):
                for part in range(2):
                    put3[s, part, pl.ds(128 * a + at, 16), :] = y[part]
            return carry

        lax.fori_loop(0, 8, close_eight, 0)

    most = pl.ds(0, 8 * (DEVICES - 1))
    for s in range(3):
        here(put3.at[s, :, most, :], got2.at[s, :, most, :], send2.at[s], recv2.at[s]).wait_recv()
        inner(s)
        got3[s, :, me] = put3[s, :, mine, :]
        everyone(
            lambda to, device: remote(
                put3.at[s, :, pl.ds(pl.multiple_of(8 * to, 8), 8), :],
                got3.at[s, :, me],
                send3.at[s],
                recv3.at[s],
                device,
            ).start()
        )

    def outer_backward(s, h):
        columns = []
        for j in range(2):
            s8 = 2 * h + j
            z = (
                rows3[pl.ds((s * 2) * 1024 + s8, 128, stride=8), :],
                rows3[pl.ds((s * 2 + 1) * 1024 + s8, 128, stride=8), :],
            )
            z = times_conj(z, (outer_turn[s, s8, 0], outer_turn[s, s8, 1]))
            columns.append(jnp.concatenate(z, axis=0))
        return left(last[s, 0], last[s, 1], jnp.concatenate(columns, axis=1))

    def wait3(s):
        here(
            put2.at[s, :, some], got3.at[s, :, some], send3.at[s], recv3.at[s]
        ).wait_recv()

    for s in range(2):
        wait3(s)

        def keep(h, carry):
            held[s, h] = outer_backward(s, h)
            return carry

        lax.fori_loop(0, 4, keep, 0)

    wait3(2)
    own_out = []
    for t in range(2):
        def finish(g, carry):
            h = 2 * t + g
            y0, y1, y2 = held[0, h], held[1, h], outer_backward(2, h)
            u, v = y1 + y2, HALF_ROOT3 * (y1 - y2)
            y = y0 - 0.5 * u
            re, im, vr, vi = y[:128], y[128:], v[:128], v[128:]
            for upper, out in enumerate(((re + vi, im - vr), (re - vi, im + vr))):
                for part in range(2):
                    for j in range(2):
                        for e in range(2):
                            at = ((part * 2 + t) * 128 + upper * 64) * 8 + (g * 2 + j) * 2 + e
                            rows4[pl.ds(at, 64, stride=8), :] = out[part][
                                64 * e : 64 * e + 64, 128 * j : 128 * j + 128
                            ]
            return carry

        lax.fori_loop(0, 2, finish, 0)
        own = pltpu.make_async_copy(put4.at[:, t, me], o_ref.at[:, me, t], own_sem.at[1 + t])
        own.start()
        own_out.append(own)
        everyone(
            lambda to, device: remote(
                put4.at[:, t, to], o_ref.at[:, me, t], send4.at[t], recv4.at[t], device
            ).start()
        )

    for own in own_out:
        own.wait()
    here(x_ref.at[:, some], got1.at[:, :, some], send1, recv1).wait_send()
    for s in range(3):
        here(put2.at[s, :, some], got3.at[s, :, some], send2.at[s], recv3.at[s]).wait_send()
        here(put2.at[s, :, some], got3.at[s, :, some], send3.at[s], recv3.at[s]).wait_send()
    for t in range(2):
        here(put4.at[:, t, some], o_ref.at[:, some, t], send4.at[t], recv4.at[t]).wait()


def solution(mesh):
    constants = tables()

    def on_device(modes):
        x = modes.reshape(2, 2, 1024, 128).transpose(0, 2, 1, 3).reshape(2, 128, 2, 8, 128)
        anywhere = pl.BlockSpec(memory_space=pl.ANY)
        dma = pltpu.SemaphoreType.DMA
        out = pl.pallas_call(
            kernel,
            out_shape=jax.ShapeDtypeStruct((2, 128, 2, 8, 128), F32),
            in_specs=[anywhere] * 5,
            out_specs=anywhere,
            scratch_shapes=[
                pltpu.VMEM((3, 2, 256, 256), BF16),
                pltpu.VMEM((3, 2, 256, 256), BF16),
                pltpu.VMEM((2, 2, 256, 256), BF16),
                pltpu.VMEM((6, 2, 128, 128), F32),
                pltpu.VMEM((2, 2, 128, 8, 128), F32),
                pltpu.VMEM((3, 2, 128, 8, 128), F32),
                pltpu.VMEM((3, 2, 1024, 128), F32),
                pltpu.VMEM((3, 2, 1024, 128), F32),
                pltpu.VMEM((3, 2, 128, 8, 128), F32),
                pltpu.VMEM((2, 2, 128, 8, 128), F32),
                pltpu.VMEM((3, 8, 2, 128, 128), F32),
                pltpu.VMEM((8, 2, 128, 128), F32),
                pltpu.VMEM((8, 2, 128, 128), F32),
                pltpu.VMEM((8, 256, 128), BF16),
                pltpu.VMEM((8, 256, 128), BF16),
                pltpu.VMEM((8, 2, 128, 128), F32),
                pltpu.VMEM((2, 4, 256, 256), F32),
                dma((4,)),
                dma((3,)),
                dma,
                dma,
                dma((3,)),
                dma((3,)),
                dma((3,)),
                dma((3,)),
                dma((2,)),
                dma((2,)),
            ],
            compiler_params=pltpu.CompilerParams(
                collective_id=0, has_side_effects=True, vmem_limit_bytes=56 * 2**20
            ),
        )(x, *(jnp.asarray(c) for c in constants))
        return out.reshape(2, 1024, 2, 128).transpose(0, 2, 1, 3).reshape(2, 2, LOCAL)

    spec = P(None, "res", "blk")
    return jax.shard_map(on_device, mesh=mesh, in_specs=(spec,), out_specs=spec, check_vma=False)
```

time: 485 us -> 143 us (0.29); the launches traced: 475 us -> 143 us
  waiting for transfers between devices: 200 us -> 0 us
  Pallas kernels: 0 us -> 140 us
  other arithmetic: 77.8 us -> 0 us
  blocking collectives: 71.5 us -> 0 us
  matrix products: 56 us -> 0 us
  local copies, waits for them, and re-layouts: 40.2 us -> 3.05 us
  starting transfers between devices: 15.7 us -> 0 us
  between operations: 14 us -> 0.01 us
    pallas_call x0 -> x1, Pallas kernels: none -> 140 us  [on_device(): pl.pallas_call(kernel, out_shape=jax.ShapeDtypeStruct((2, 128, 2, 8, 128)...]
    reduce_scatter x2 -> x0, waiting for transfers between devices: 83.3 us -> none  [own_block(): tiles = lax.psum_scatter(tiles, axes[k], scatter_dimension=0, tiled=True)]
    all_to_all x2 -> x0, blocking collectives: 71.5 us -> none  [the longest x1 36.9 us: on_device(): lax.all_to_all(modes.reshape(2, 2, blocks, narrow), 'blk', split_axis=2,...]
    all_gather x1 -> x0, waiting for transfers between devices: 59.3 us -> none  [on_device(): every = lax.all_gather(moved_in, RES, axis=1, tiled=True)]
    all_to_all x2 -> x0, waiting for transfers between devices: 57.5 us -> none  [the longest x1 39 us: on_device(): lax.all_to_all(local.reshape(2, 3, blocks, narrow), 'blk', split_axis=2,...]
    dot_general x6 -> x0, matrix products: 56 us -> none  [the longest x1 20.9 us: on_device(): jnp.einsum('akbj,bxsj->axsk', inner_pair[0], local, precision=highest)]
    sub x8 -> x0, other arithmetic: 46.6 us -> none  [the longest x7 46.1 us: times(): left[0] * right[0] - left[1] * right[1]]
    all_to_all x2 -> x0, starting transfers between devices: 15.6 us -> none  [the longest x1 8.37 us: on_device(): lax.all_to_all(local.reshape(2, 3, blocks, narrow), 'blk', split_axis=2,...]
  transfers between devices with their start and end apart: 5 -> 0, of which waited for: 5 -> 0; matrix products, arithmetic and copies ran while one was open for 5% -> 0% of each run, Pallas kernels for 0% -> 0%
where the time goes in v1:
time: 143 us
  Pallas kernels  140 us (98%)
  local copies, waits for them, and re-layouts  3.05 us (2%)
    pallas_call x1, Pallas kernels, on_device(): pl.pallas_call(kernel, out_shape=jax.ShapeDtypeStruct((2, 128, 2, 8, 128)...  140 us
    unnamed x1, local copies, waits for them, and re-layouts  3.05 us

profile of v1, /device:TPU:0, one launch (start us, length us, event | category | flops | bytes accessed | tf_op | source)
XLA Modules:
  0.0 142.9 jit_solution(5710043315962374524)
XLA Ops:
  0.0 139.8 %shard_map.55 = f32[2,128,2,8,128]{4,3,2,1,0:T(8,128)} custom-call(f32[2,128,2,8,128]{4,3,2,1,0:T(8,128)} %bitcast.11, bf16[3,2,256,256]{3,2,1,0:T(8,128)(2,1)} %constant.8.clone.first_hbm, bf16[3,2,256,256]{3,2,1,0:T(8,128)(2,1)} %constant.9.clone.last_hbm, bf16[2,2,256,256]{3,2,1,0:T(8,128)(2,1)} %constant.10.clone.fg_hbm, ...), custom_call_target="tpu_custom_call" | custom-call | tf_op jit(solution)/shard_map/pallas_call | solution.py:404
  139.8 3.0 %copy.9 = f32[2,2,131072]{2,1,0:T(2,128)} copy(f32[2,2,131072]{2,1,0:T(2,128)} %bitcast.10) | data formatting | bytes 4194304

commit v2 on v1

--- a/solution.py
+++ b/solution.py
@@ -40,11 +40,12 @@
         w = root(np.outer(n, kl) / 128.0) * root(kl * s / 384.0)[None, :]
         first.append(high_low(real_block(w)))
         last.append(high_low(real_block(w).T / PADDED))
-    f = real_block(root(np.outer(n, n) / 128.0))
+    mixed = (n % 64) // 4 * 8 + n // 64 * 4 + n % 4
+    f = real_block(root(np.outer(n, mixed) / 128.0))
     turn = [root(np.outer(3 * n + s, n) / PADDED) for s in range(3)]
     turn.append(root(np.outer(n, n) / 16384.0))
     columns = np.zeros((128, 128), np.complex128)
-    columns[:, :8] = root(np.outer(n, np.arange(8)) / 1024.0)
+    columns[:, :8] = root(np.outer(mixed, np.arange(8)) / 1024.0)
     turn.append(columns)
     rows = np.zeros((128, 128), np.complex128)
     rows[:8] = root(np.outer(np.arange(8), n) / LOCAL)
@@ -124,7 +125,7 @@
     x_ref, first_hbm, last_hbm, fg_hbm, turn_hbm, o_ref,
     first, last, fg, turn, got1, put2, got2, put3, got3, put4,
     outer_turn, column_turn, inner_turn, high, low, back, held,
-    const_sem, own_sem, send1, recv1, send2, recv2, send3, recv3, send4, recv4,
+    near_sem, const_sem, own_sem, send1, recv1, send2, recv2, send3, recv3, send4, recv4,
 ):
     r, b = lax.axis_index("res"), lax.axis_index("blk")
     me = r * 32 + b
@@ -139,22 +140,6 @@
         copy.start()
     own_in = pltpu.make_async_copy(x_ref.at[:, me], got1.at[:, :, me], own_sem.at[0])
     own_in.start()
-
-    def everyone(body):
-        def step(i, carry):
-            to = (me + i * STEP) % DEVICES
-            body(to, {"res": to // 32, "blk": to % 32})
-            return carry
-
-        lax.fori_loop(1, DEVICES, step, 0)
-
-    barrier = pltpu.get_barrier_semaphore()
-    everyone(
-        lambda to, device: pl.semaphore_signal(
-            barrier, inc=1, device_id=device, device_id_type=MESH
-        )
-    )
-    pl.semaphore_wait(barrier, DEVICES - 1)
 
     def remote(src, dst, send, recv, device):
         return pltpu.make_async_remote_copy(
@@ -169,9 +154,92 @@
     def here(src, dst, send, recv):
         return remote(src, dst, send, recv, {"res": r, "blk": b})
 
+    def everyone(body):
+        def step(i, carry):
+            to = (me + i * STEP) % DEVICES
+            body(to, {"res": to // 32, "blk": to % 32})
+            return carry
+
+        lax.fori_loop(1, DEVICES, step, 0)
+
+    at_x, at_y, at_z, at_core = r // 2 * 2 + b // 16, b // 4 % 4, b % 4, r % 2
+
+    def away(body, x=0, y=0, z=0, core=0):
+        to_x = (at_x + x) % 4
+        res = to_x // 2 * 2 + (at_core + core) % 2
+        blk = to_x % 2 * 16 + (at_y + y) % 4 * 4 + (at_z + z) % 4
+        body(res * 32 + blk, {"res": res, "blk": blk})
+
+    def loop(count, body):
+        def step(i, carry):
+            body(i)
+            return carry
+
+        lax.fori_loop(0, count, step, 0)
+
+    def one(body):
+        def step(i):
+            away(body, x=1 + i)
+            away(body, y=1 + i)
+            away(body, z=1 + i)
+
+        loop(3, step)
+        away(body, core=1)
+
+    def two(body):
+        def step(i):
+            p, q = 1 + i % 3, 1 + i // 3
+            away(body, x=p, y=q)
+            away(body, y=p, z=q)
+            away(body, z=p, x=q)
+
+        loop(9, step)
+
+        def over(i):
+            away(body, x=1 + i, core=1)
+            away(body, y=1 + i, core=1)
+            away(body, z=1 + i, core=1)
+
+        loop(3, over)
+
+    def three(body):
+        def step(i):
+            p, q = 1 + i % 3, 1 + i // 3
+            for u in range(3):
+                away(body, x=p, y=q, z=1 + u)
+            away(body, x=p, y=q, core=1)
+            away(body, y=p, z=q, core=1)
+            away(body, z=p, x=q, core=1)
+
+        loop(9, step)
+
+    def four_apart(body):
+        def step(i):
+            p, q = 1 + i % 3, 1 + i // 3
+            for u in range(3):
+                away(body, x=p, y=q, z=1 + u, core=1)
+
+        loop(9, step)
+
+    barrier = pltpu.get_barrier_semaphore()
+
+    def first_half(to, device):
+        remote(x_ref.at[:, to, 0], got1.at[:, 0, me], send1, recv1.at[0], device).start()
+
+    rounds = (barrier, near_sem.at[0], near_sem.at[1], near_sem.at[2])
+    for k, group in enumerate((None, one, two, three)):
+        one(
+            lambda to, device: pl.semaphore_signal(
+                rounds[k], inc=1, device_id=device, device_id_type=MESH
+            )
+        )
+        if group is not None:
+            group(first_half)
+        pl.semaphore_wait(rounds[k], 10)
+    four_apart(first_half)
     everyone(
         lambda to, device: remote(
-            x_ref.at[:, to], got1.at[:, :, me], send1, recv1, device
+            x_ref.at[:, to, 1], got1.at[:, 1, me], send1, recv1.at[1], device
         ).start()
     )
 
@@ -207,22 +275,24 @@
 
     own_in.wait()
     some = pl.ds(0, DEVICES - 1)
-    here(x_ref.at[:, some], got1.at[:, :, some], send1, recv1).wait_recv()
 
     rows1 = got1.reshape(2 * 2 * 128 * 8, 128)
     rows2 = put2.reshape(3 * 2 * 128 * 8, 128)
+    from2 = got2.reshape(3 * 2 * 128 * 8, 128)
+    rows_out = put3.reshape(3 * 2 * 128 * 8, 128)
     rows3 = got3.reshape(3 * 2 * 128 * 8, 128)
     rows4 = put4.reshape(2 * 2 * 128 * 8, 128)
 
-    def outer_forward(s):
+    def outer_forward(s, t):
         cr = (1.0, -0.5, -0.5)[s]
         ci = (0.0, HALF_ROOT3, -HALF_ROOT3)[s]
 
-        def body(h, carry):
+        def body(g, carry):
+            h = 2 * t + g
             columns = []
             for j in range(2):
                 def block(part, upper):
-                    at = ((part * 2 + h // 2) * 128 + upper * 64) * 8 + ((h % 2) * 2 + j) * 2
+                    at = ((part * 2 + t) * 128 + upper * 64) * 8 + (g * 2 + j) * 2
                     return jnp.concatenate(
                         [rows1[pl.ds(at + e, 64, stride=8), :] for e in range(2)], axis=0
                     )
@@ -241,27 +311,47 @@
                 s8 = 2 * h + j
                 part = (out[:128, 128 * j : 128 * j + 128], out[128:, 128 * j : 128 * j + 128])
                 re, im = times(part, (outer_turn[s, s8, 0], outer_turn[s, s8, 1]))
-                rows2[pl.ds((s * 2) * 1024 + s8, 128, stride=8), :] = re
-                rows2[pl.ds((s * 2 + 1) * 1024 + s8, 128, stride=8), :] = im
-            return carry
-
-        lax.fori_loop(0, 4, body, 0)
-
-    mine = pl.ds(pl.multiple_of(8 * me, 8), 8)
-    for s in range(3):
-        outer_forward(s)
-        got2[s, :, mine, :] = put2[s, :, me]
+                at = (s * 2 + t) * 1024 + (g * 2 + j) * 2
+                rows2[pl.ds(at, 128, stride=8), :] = re
+                rows2[pl.ds(at + 1, 128, stride=8), :] = im
+            return carry
+
+        lax.fori_loop(0, 2, body, 0)
+
+    def wait1(t):
+        here(x_ref.at[:, some, t], got1.at[:, t, some], send1, recv1.at[t]).wait_recv()
+
+    def give2(s, t):
+        got2[s, t, me] = put2[s, t, me]
         everyone(
             lambda to, device: remote(
-                put2.at[s, :, to], got2.at[s, :, mine, :], send2.at[s], recv2.at[s], device
+                put2.at[s, t, to], got2.at[s, t, me], send2, recv2.at[s], device
             ).start()
         )
+
+    def give2_both(s):
+        got2[s, :, me] = put2[s, :, me]
+        everyone(
+            lambda to, device: remote(
+                put2.at[s, :, to], got2.at[s, :, me], send2, recv2.at[s], device
+            ).start()
+        )
+
+    for t in range(2):
+        wait1(t)
+        outer_forward(0, t)
+        give2(0, t)
+    for s in (1, 2):
+        outer_forward(s, 0)
+        outer_forward(s, 1)
+        give2_both(s)
 
     def inner(s):
         def open_eight(i, carry):
             at = pl.multiple_of(16 * i, 16)
+            start = (s * 2 + i // 4) * 1024 + i % 4 * 32
             v = [
-                (got2[s, 0, pl.ds(128 * a + at, 16), :], got2[s, 1, pl.ds(128 * a + at, 16), :])
+                tuple(from2[pl.ds(start + 128 * a + part, 16, stride=2), :] for part in range(2))
                 for a in range(8)
             ]
             for a, y in enumerate(eight(v, 1)):
@@ -283,17 +373,17 @@
             lines = []
             for j, a in enumerate(pair):
                 y = (out[:128, 128 * j : 128 * j + 128], out[128:, 128 * j : 128 * j + 128])
-                lines.append(jnp.concatenate(times(y, (inner_turn[a, 0], inner_turn[a, 1])), axis=1))
-            v = right(jnp.concatenate(lines, axis=0), fg[1, 0], fg[1, 1])
+                re, im = times(y, (inner_turn[a, 0], inner_turn[a, 1]))
+                lines.append(jnp.concatenate((re, -im), axis=1))
+            v = right(jnp.concatenate(lines, axis=0), fg[0, 0], fg[0, 1])
             re, im = v[:, :128], v[:, 128:]
             squared = jnp.concatenate([(re + im) * (re - im), 2.0 * re * im], axis=1)
-            v = right(squared, fg[0, 0], fg[0, 1])
+            v = right(squared, fg[1, 0], fg[1, 1])
             columns = []
             for j, a in enumerate(pair):
                 y = (v[128 * j : 128 * j + 128, :128], v[128 * j : 128 * j + 128, 128:])
-                columns.append(
-                    jnp.concatenate(times_conj(y, (inner_turn[a, 0], inner_turn[a, 1])), axis=0)
-                )
+                re, im = times(y, (inner_turn[a, 0], inner_turn[a, 1]))
+                columns.append(jnp.concatenate((re, -im), axis=0))
             out = left(fg[1, 0], fg[1, 1], jnp.concatenate(columns, axis=1))
             for j, a in enumerate(pair):
                 y = (out[:128, 128 * j : 128 * j + 128], out[128:, 128 * j : 128 * j + 128])
@@ -306,48 +396,45 @@
 
         def close_eight(i, carry):
             at = pl.multiple_of(16 * i, 16)
+            start = (s * 2 + i // 4) * 1024 + i % 4 * 32
             v = [(back[a, 0, pl.ds(at, 16), :], back[a, 1, pl.ds(at, 16), :]) for a in range(8)]
             for a, y in enumerate(eight(v, -1)):
                 for part in range(2):
-                    put3[s, part, pl.ds(128 * a + at, 16), :] = y[part]
+                    rows_out[pl.ds(start + 128 * a + part, 16, stride=2), :] = y[part]
             return carry
 
         lax.fori_loop(0, 8, close_eight, 0)
 
-    most = pl.ds(0, 8 * (DEVICES - 1))
     for s in range(3):
-        here(put3.at[s, :, most, :], got2.at[s, :, most, :], send2.at[s], recv2.at[s]).wait_recv()
+        here(put2.at[s, :, some], got2.at[s, :, some], send2, recv2.at[s]).wait_recv()
         inner(s)
-        got3[s, :, me] = put3[s, :, mine, :]
-        everyone(
-            lambda to, device: remote(
-                put3.at[s, :, pl.ds(pl.multiple_of(8 * to, 8), 8), :],
-                got3.at[s, :, me],
-                send3.at[s],
-                recv3.at[s],
-                device,
-            ).start()
-        )
+        got3[s, :, me] = put3[s, :, me]
+        if s < 2:
+            everyone(
+                lambda to, device: remote(
+                    put3.at[s, :, to], got3.at[s, :, me], send3, recv3.at[s], device
+                ).start()
+            )
+        else:
+            for t in range(2):
+                everyone(
+                    lambda to, device: remote(
+                        put3.at[s, t, to], got3.at[s, t, me], send3, recv3.at[s + t], device
+                    ).start()
+                )
 
     def outer_backward(s, h):
         columns = []
         for j in range(2):
             s8 = 2 * h + j
-            z = (
-                rows3[pl.ds((s * 2) * 1024 + s8, 128, stride=8), :],
-                rows3[pl.ds((s * 2 + 1) * 1024 + s8, 128, stride=8), :],
-            )
+            at = (s * 2 + h // 2) * 1024 + (h % 2 * 2 + j) * 2
+            z = tuple(rows3[pl.ds(at + part, 128, stride=8), :] for part in range(2))
             z = times_conj(z, (outer_turn[s, s8, 0], outer_turn[s, s8, 1]))
             columns.append(jnp.concatenate(z, axis=0))
         return left(last[s, 0], last[s, 1], jnp.concatenate(columns, axis=1))
 
-    def wait3(s):
-        here(
-            put2.at[s, :, some], got3.at[s, :, some], send3.at[s], recv3.at[s]
-        ).wait_recv()
-
     for s in range(2):
-        wait3(s)
+        here(put3.at[s, :, some], got3.at[s, :, some], send3, recv3.at[s]).wait_recv()
 
         def keep(h, carry):
             held[s, h] = outer_backward(s, h)
@@ -355,9 +442,10 @@
 
         lax.fori_loop(0, 4, keep, 0)
 
-    wait3(2)
     own_out = []
     for t in range(2):
+        here(put3.at[2, t, some], got3.at[2, t, some], send3, recv3.at[2 + t]).wait_recv()
+
         def finish(g, carry):
             h = 2 * t + g
             y0, y1, y2 = held[0, h], held[1, h], outer_backward(2, h)
@@ -380,18 +468,24 @@
         own_out.append(own)
         everyone(
             lambda to, device: remote(
-                put4.at[:, t, to], o_ref.at[:, me, t], send4.at[t], recv4.at[t], device
+                put4.at[:, t, to], o_ref.at[:, me, t], send4, recv4.at[t], device
             ).start()
         )
 
     for own in own_out:
         own.wait()
-    here(x_ref.at[:, some], got1.at[:, :, some], send1, recv1).wait_send()
+    here(x_ref.at[:, some], got1.at[:, :, some], send1, recv1.at[0]).wait_send()
     for s in range(3):
-        here(put2.at[s, :, some], got3.at[s, :, some], send2.at[s], recv3.at[s]).wait_send()
-        here(put2.at[s, :, some], got3.at[s, :, some], send3.at[s], recv3.at[s]).wait_send()
+        here(put2.at[s, :, some], got2.at[s, :, some], send2, recv2.at[s]).wait_send()
+        here(put3.at[s, :, some], got3.at[s, :, some], send3, recv3.at[s]).wait_send()
     for t in range(2):
-        here(put4.at[:, t, some], o_ref.at[:, some, t], send4.at[t], recv4.at[t]).wait()
+        here(put4.at[:, t, some], o_ref.at[:, some, t], send4, recv4.at[t]).wait()
+
+
+def hand_over(in_ref, o_ref, sem):
+    copy = pltpu.make_async_copy(in_ref, o_ref, sem)
+    copy.start()
+    copy.wait()
 
 
 def solution(mesh):
@@ -403,9 +497,9 @@
         dma = pltpu.SemaphoreType.DMA
         out = pl.pallas_call(
             kernel,
-            out_shape=jax.ShapeDtypeStruct((2, 128, 2, 8, 128), F32),
+            out_shape=pltpu.VMEM((2, 128, 2, 8, 128), F32),
             in_specs=[anywhere] * 5,
-            out_specs=anywhere,
+            out_specs=pl.BlockSpec(memory_space=pltpu.VMEM),
             scratch_shapes=[
                 pltpu.VMEM((3, 2, 256, 256), BF16),
                 pltpu.VMEM((3, 2, 256, 256), BF16),
@@ -413,8 +507,8 @@
                 pltpu.VMEM((6, 2, 128, 128), F32),
                 pltpu.VMEM((2, 2, 128, 8, 128), F32),
                 pltpu.VMEM((3, 2, 128, 8, 128), F32),
-                pltpu.VMEM((3, 2, 1024, 128), F32),
-                pltpu.VMEM((3, 2, 1024, 128), F32),
+                pltpu.VMEM((3, 2, 128, 8, 128), F32),
+                pltpu.VMEM((3, 2, 128, 8, 128), F32),
                 pltpu.VMEM((3, 2, 128, 8, 128), F32),
                 pltpu.VMEM((2, 2, 128, 8, 128), F32),
                 pltpu.VMEM((3, 8, 2, 128, 128), F32),
@@ -424,21 +518,30 @@
                 pltpu.VMEM((8, 256, 128), BF16),
                 pltpu.VMEM((8, 2, 128, 128), F32),
                 pltpu.VMEM((2, 4, 256, 256), F32),
+                pltpu.SemaphoreType.REGULAR((3,)),
                 dma((4,)),
                 dma((3,)),
                 dma,
+                dma((2,)),
                 dma,
                 dma((3,)),
-                dma((3,)),
-                dma((3,)),
-                dma((3,)),
-                dma((2,)),
+                dma,
+                dma((4,)),
+                dma,
                 dma((2,)),
             ],
             compiler_params=pltpu.CompilerParams(
-                collective_id=0, has_side_effects=True, vmem_limit_bytes=56 * 2**20
+                collective_id=0, has_side_effects=True, vmem_limit_bytes=67043328 - 2**21 - 2**17
             ),
         )(x, *(jnp.asarray(c) for c in constants))
+        out = pl.pallas_call(
+            hand_over,
+            out_shape=jax.ShapeDtypeStruct((2, 128, 2, 8, 128), F32),
+            in_specs=[pl.BlockSpec(memory_space=pltpu.VMEM)],
+            out_specs=anywhere,
+            scratch_shapes=[dma],
+            compiler_params=pltpu.CompilerParams(vmem_limit_bytes=2**17),
+        )(out)
         return out.reshape(2, 1024, 2, 128).transpose(0, 2, 1, 3).reshape(2, 2, LOCAL)
 
     spec = P(None, "res", "blk")

time: 143 us -> 129 us (0.902)
  Pallas kernels: 140 us -> 128 us
  local copies, waits for them, and re-layouts: 3.05 us -> 0 us
    pallas_call x1 -> x2, Pallas kernels: 140 us -> 128 us  [the longest x1 127 us: on_device(): pl.pallas_call(kernel, out_shape=pltpu.VMEM((2, 128, 2, 8, 128), F32), in...]
    unnamed x1 -> x0, local copies, waits for them, and re-layouts: 3.05 us -> none
where the time goes in v2:
time: 129 us; the launch traced here: 128 us
  Pallas kernels  128 us (99%)
    pallas_call x1, Pallas kernels, on_device(): pl.pallas_call(kernel, out_shape=pltpu.VMEM((2, 128, 2, 8, 128), F32), in...  127 us

profile of v2, /device:TPU:0, one launch (start us, length us, event | category | flops | bytes accessed | tf_op | source)
XLA Modules:
  0.0 127.9 jit_solution(5288111061414914632)
XLA Ops:
  0.0 126.6 %shard_map.55.in_ref = f32[2,128,2,8,128]{4,3,2,1,0:T(8,128)S(1)} custom-call(f32[2,128,2,8,128]{4,3,2,1,0:T(8,128)} %bitcast.10, bf16[3,2,256,256]{3,2,1,0:T(8,128)(2,1)} %constant.8.clone.first_hbm, bf16[3,2,256,256]{3,2,1,0:T(8,128)(2,1)} %constant.9.clone.last_hbm, bf16[2,2,256,256]{3,2,1,0:T(8,128)(2,1)} %constant.10.clone.fg_hbm, ...), custom_call_target="tpu_custom_call" | custom-call | tf_op jit(solution)/shard_map/pallas_call | solution.py:498
  126.6 1.3 %shard_map.56 = f32[2,128,2,8,128]{4,3,2,1,0:T(8,128)} custom-call(f32[2,128,2,8,128]{4,3,2,1,0:T(8,128)S(1)} %shard_map.55.in_ref), custom_call_target="tpu_custom_call" | custom-call | tf_op jit(solution)/shard_map/pallas_call | solution.py:537

commit v3 on v2

--- a/solution.py
+++ b/solution.py
@@ -337,14 +337,18 @@
             ).start()
         )
 
+    wait1(0)
+    for s in range(2):
+        outer_forward(s, 0)
+        give2(s, 0)
+    wait1(1)
+    outer_forward(0, 1)
+    give2(0, 1)
+    outer_forward(1, 1)
+    give2(1, 1)
     for t in range(2):
-        wait1(t)
-        outer_forward(0, t)
-        give2(0, t)
-    for s in (1, 2):
-        outer_forward(s, 0)
-        outer_forward(s, 1)
-        give2_both(s)
+        outer_forward(2, t)
+        give2(2, t)
 
     def inner(s):
         def open_eight(i, carry):

time: 129 us -> 128 us (level); the launches traced: 128 us -> 128 us
  no operation moved by 1% of the time
where the time goes in v3:
time: 128 us
  Pallas kernels  128 us (100%)
    pallas_call x1, Pallas kernels, on_device(): pl.pallas_call(kernel, out_shape=pltpu.VMEM((2, 128, 2, 8, 128), F32), in...  127 us

profile of v3, /device:TPU:0, one launch (start us, length us, event | category | flops | bytes accessed | tf_op | source)
XLA Modules:
  0.0 128.3 jit_solution(9518629933664337848)
XLA Ops:
  0.0 127.0 %shard_map.55.in_ref = f32[2,128,2,8,128]{4,3,2,1,0:T(8,128)S(1)} custom-call(f32[2,128,2,8,128]{4,3,2,1,0:T(8,128)} %bitcast.10, bf16[3,2,256,256]{3,2,1,0:T(8,128)(2,1)} %constant.8.clone.first_hbm, bf16[3,2,256,256]{3,2,1,0:T(8,128)(2,1)} %constant.9.clone.last_hbm, bf16[2,2,256,256]{3,2,1,0:T(8,128)(2,1)} %constant.10.clone.fg_hbm, ...), custom_call_target="tpu_custom_call" | custom-call | tf_op jit(solution)/shard_map/pallas_call | solution.py:502
  127.0 1.3 %shard_map.56 = f32[2,128,2,8,128]{4,3,2,1,0:T(8,128)} custom-call(f32[2,128,2,8,128]{4,3,2,1,0:T(8,128)S(1)} %shard_map.55.in_ref), custom_call_target="tpu_custom_call" | custom-call | tf_op jit(solution)/shard_map/pallas_call | solution.py:541

commit v4 on v3

--- a/solution.py
+++ b/solution.py
@@ -136,10 +136,7 @@
             ((first_hbm, first), (last_hbm, last), (fg_hbm, fg), (turn_hbm, turn))
         )
     ]
-    for copy in constants:
-        copy.start()
     own_in = pltpu.make_async_copy(x_ref.at[:, me], got1.at[:, :, me], own_sem.at[0])
-    own_in.start()
 
     def remote(src, dst, send, recv, device):
         return pltpu.make_async_remote_copy(
@@ -235,6 +232,10 @@
         )
         if group is not None:
             group(first_half)
+        else:
+            for copy in constants:
+                copy.start()
+            own_in.start()
         pl.semaphore_wait(rounds[k], 10)
     four_apart(first_half)
     everyone(

time: 128 us -> 128 us (level)
  no operation moved by 1% of the time
where the time goes in v4:
time: 128 us
  Pallas kernels  128 us (100%)
    pallas_call x1, Pallas kernels, on_device(): pl.pallas_call(kernel, out_shape=pltpu.VMEM((2, 128, 2, 8, 128), F32), in...  127 us

profile of v4, /device:TPU:0, one launch (start us, length us, event | category | flops | bytes accessed | tf_op | source)
XLA Modules:
  0.0 128.2 jit_solution(5449438561312838264)
XLA Ops:
  0.0 126.9 %shard_map.55.in_ref = f32[2,128,2,8,128]{4,3,2,1,0:T(8,128)S(1)} custom-call(f32[2,128,2,8,128]{4,3,2,1,0:T(8,128)} %bitcast.10, bf16[3,2,256,256]{3,2,1,0:T(8,128)(2,1)} %constant.8.clone.first_hbm, bf16[3,2,256,256]{3,2,1,0:T(8,128)(2,1)} %constant.9.clone.last_hbm, bf16[2,2,256,256]{3,2,1,0:T(8,128)(2,1)} %constant.10.clone.fg_hbm, ...), custom_call_target="tpu_custom_call" | custom-call | tf_op jit(solution)/shard_map/pallas_call | solution.py:503
  126.9 1.3 %shard_map.56 = f32[2,128,2,8,128]{4,3,2,1,0:T(8,128)} custom-call(f32[2,128,2,8,128]{4,3,2,1,0:T(8,128)S(1)} %shard_map.55.in_ref), custom_call_target="tpu_custom_call" | custom-call | tf_op jit(solution)/shard_map/pallas_call | solution.py:542
